TPU v7x, 32 devices: a whole 2x2x4 slice. The times are simulated.
32 devices in a mesh: dp: 4 (over x, core), pipe: 2 (over y), tensor: 4 (over z).
Axes of the slice: x: 2, y: 2, z: 4, core: 2. Of those that a mesh axis runs over, the one named last changes fastest.
Arguments:
- weights: bfloat16 [2816, 1408], P(('dp', 'pipe', 'tensor')), may hold values from -6 to 6
- first_moment: bfloat16 [2816, 1408], P(('dp', 'pipe', 'tensor')), may hold values from -6 to 6
- second_moment: bfloat16 [2816, 1408], P(('dp', 'pipe', 'tensor')), may hold values from 0.049804688 to 5
- row_weight: float32 [1408], replicated, may hold values from -1 to 1
- col_weight: float32 [1408], replicated, may hold values from 1 to 4
Outputs:
- weight_tiles: bfloat16 [2816, 1408], P(('pipe', 'tensor'))
- first_tiles: bfloat16 [2816, 1408], P(('pipe', 'tensor'))
- second_tiles: bfloat16 [2816, 1408], P(('pipe', 'tensor'))
- checksums: float32 [3, 2, 4, 11], P(None, 'pipe', 'tensor')
All inputs are finite; a program needn't handle non-finite values.
Results may differ from a plain program's by a relative error of at most 0.001.
Values may be sent and summed in bfloat16 or wider, within the bound.
A program may use at most 64 MiB of HBM per device.

v0:
```python
import jax
import jax.numpy as jnp
from jax import lax
from jax.sharding import PartitionSpec as P

CHECK_COLS = 128


def for_sending(array):
    return jax.tree.map(lambda a: a.astype(jnp.bfloat16) if a.dtype == jnp.float32 else a, array)


def column_sums(data, row_part, col_weight, col_blocks):
    row_mixed = jnp.dot(
        row_part[None, :], data.astype(jnp.float32), precision=lax.Precision.HIGHEST
    )[0]
    return jnp.sum((row_mixed * col_weight).reshape(col_blocks, -1), axis=1)


def shards(weights, first_moment, second_moment, row_weight, col_weight):
    dp_count = lax.axis_size("dp")
    pipe_count = lax.axis_size("pipe")
    tensor_count = lax.axis_size("tensor")
    shard_rows, width = weights.shape
    dp_section = dp_count // pipe_count
    tile_shards = dp_count // tensor_count
    piece_cols = width // dp_count
    tile_rows = shard_rows * dp_count
    col_blocks = width // CHECK_COLS
    factor = float(tile_rows * CHECK_COLS) ** (-0.5)
    sources = (weights, first_moment, second_moment)
    exchanged = (
        lax.all_to_all(sources[0], "dp", split_axis=1, concat_axis=0, tiled=True),
        lax.all_to_all(sources[1], "dp", split_axis=1, concat_axis=0, tiled=True),
        lax.all_to_all(sources[2], "dp", split_axis=1, concat_axis=0, tiled=True),
    )
    grouped = tuple(
        (item.reshape(pipe_count, dp_section, shard_rows, piece_cols) for item in exchanged)
    )
    sectioned = jax.tree.map(
        lambda part, own: part.astype(own.dtype),
        lax.all_to_all(for_sending(grouped), "pipe", split_axis=0, concat_axis=2, tiled=True),
        grouped,
    )
    routed = tuple(
        (item.reshape(tensor_count, tile_shards, 1, shard_rows, piece_cols) for item in sectioned)
    )
    arrived = jax.tree.map(
        lambda part, own: part.astype(own.dtype),
        lax.all_to_all(for_sending(routed), "tensor", split_axis=0, concat_axis=2, tiled=True),
        routed,
    )
    flat_pieces = tuple((item.reshape(tile_rows, piece_cols) for item in arrived))
    tiles = jax.tree.map(
        lambda part, own: part.astype(own.dtype),
        lax.all_gather(for_sending(flat_pieces), "dp", axis=1, tiled=True),
        flat_pieces,
    )
    tensor_pos = lax.axis_index("tensor")
    flat_index = (
        lax.axis_index("dp") * pipe_count + lax.axis_index("pipe")
    ) * tensor_count + tensor_pos
    in_section = flat_index % (dp_count * tensor_count)
    section_of = flat_index // (dp_count * tensor_count)
    tile_of = in_section // dp_count
    row_part = lax.dynamic_slice_in_dim(row_weight, in_section * shard_rows, shard_rows)
    partial_value = jnp.stack(
        [column_sums(item, row_part, col_weight, col_blocks) for item in sources]
    )
    section_hit = (jnp.arange(pipe_count) == section_of).astype(jnp.float32)
    tile_hit = (jnp.arange(tensor_count) == tile_of).astype(jnp.float32)
    spread = (
        partial_value[:, None, None, :]
        * section_hit[None, :, None, None]
        * tile_hit[None, None, :, None]
    )
    summed = lax.psum(spread, ("dp", "pipe", "tensor"))
    checks = (
        lax.dynamic_slice(summed, (0, lax.axis_index("pipe"), tensor_pos, 0), (3, 1, 1, col_blocks))
        * factor
    )
    return (tiles[0], tiles[1], tiles[2], checks)


def solution(mesh):
    return jax.shard_map(
        shards,
        mesh=mesh,
        in_specs=(
            P(("dp", "pipe", "tensor"), None),
            P(("dp", "pipe", "tensor"), None),
            P(("dp", "pipe", "tensor"), None),
            P(),
            P(),
        ),
        out_specs=(
            P(("pipe", "tensor"), None),
            P(("pipe", "tensor"), None),
            P(("pipe", "tensor"), None),
            P(None, "pipe", "tensor", None),
        ),
        check_vma=False,
    )
```

profile of v0, /device:TPU:0, one launch (start us, length us, event | category | flops | bytes accessed | tf_op | source)
XLA Modules:
  0.0 154.1 jit_solution(8427268718347811385)
XLA Ops:
  0.6 0.0 copy-start
  0.6 0.0 copy-start.3
  0.7 1.3 all_to_all.90
  1.9 0.7 copy.33
  2.7 4.4 %all-to-all-start = ((bf16[88,4,352]{2,0,1:T(8,128)(2,1)}), bf16[88,4,352]{2,0,1:T(8,128)(2,1)}, u32[]{:S(2)}, u32[]{:S(2)}) async-start(bf16[88,4,352]{2,0,1:T(8,128)(2,1)} %copy.33), calls=%async_computation | async-start | bytes 540672 | tf_op jit(solution)/shard_map/all_to_all | solution.py:33
  7.0 0.0 copy-done.3
  7.0 0.3 all_to_all.97
  7.3 0.7 copy.37
  8.1 5.6 %all-to-all-done = bf16[88,4,352]{2,0,1:T(8,128)(2,1)} async-done(((bf16[88,4,352]{2,0,1:T(8,128)(2,1)}), bf16[88,4,352]{2,0,1:T(8,128)(2,1)}, u32[]{:S(2)}, u32[]{:S(2)}) %all-to-all-start) | async-done | bytes 247840 | tf_op jit(solution)/shard_map/all_to_all | solution.py:33
  13.7 4.1 %all-to-all-start.3 = ((bf16[88,4,352]{2,0,1:T(8,128)(2,1)}), bf16[88,4,352]{2,0,1:T(8,128)(2,1)}, u32[]{:S(2)}, u32[]{:S(2)}) async-start(bf16[88,4,352]{2,0,1:T(8,128)(2,1)} %copy.37), calls=%async_computation.3 | async-start | bytes 540672 | tf_op jit(solution)/shard_map/all_to_all | solution.py:34
  17.8 0.3 all_to_all.104
  18.1 0.0 copy-start.4
  18.1 0.7 copy.41
  18.9 5.1 %all-to-all-done.3 = bf16[88,4,352]{2,0,1:T(8,128)(2,1)} async-done(((bf16[88,4,352]{2,0,1:T(8,128)(2,1)}), bf16[88,4,352]{2,0,1:T(8,128)(2,1)}, u32[]{:S(2)}, u32[]{:S(2)}) %all-to-all-start.3) | async-done | bytes 247840 | tf_op jit(solution)/shard_map/all_to_all | solution.py:34
  24.0 4.1 %all-to-all-start.6 = ((bf16[88,4,352]{2,0,1:T(8,128)(2,1)}), bf16[88,4,352]{2,0,1:T(8,128)(2,1)}, u32[]{:S(2)}, u32[]{:S(2)}) async-start(bf16[88,4,352]{2,0,1:T(8,128)(2,1)} %copy.41), calls=%async_computation.6 | async-start | bytes 540672 | tf_op jit(solution)/shard_map/all_to_all | solution.py:35
  28.1 0.3 convolution_reduce_fusion.2
  28.4 0.3 convolution_reduce_fusion
  28.7 5.5 %all-to-all-done.6 = bf16[88,4,352]{2,0,1:T(8,128)(2,1)} async-done(((bf16[88,4,352]{2,0,1:T(8,128)(2,1)}), bf16[88,4,352]{2,0,1:T(8,128)(2,1)}, u32[]{:S(2)}, u32[]{:S(2)}) %all-to-all-start.6) | async-done | bytes 247840 | tf_op jit(solution)/shard_map/all_to_all | solution.py:35
  34.2 3.6 %all-to-all-start.1 = ((bf16[2,2,88,352]{3,2,1,0:T(8,128)(2,1)}), bf16[2,2,88,352]{3,2,1,0:T(8,128)(2,1)S(1)}, u32[]{:S(2)}, u32[]{:S(2)}) async-start(bf16[2,2,88,352]{3,2,1,0:T(8,128)(2,1)} %bitcast.1), calls=%async_computation.1 | async-start | bytes 540672 | tf_op jit(solution)/shard_map/all_to_all | solution.py:42
  37.8 0.3 convolution_reduce_fusion.1
  38.1 0.1 bitcast_reduce_fusion.2
  38.3 5.2 %all-to-all-done.1 = bf16[2,2,88,352]{3,2,1,0:T(8,128)(2,1)S(1)} async-done(((bf16[2,2,88,352]{3,2,1,0:T(8,128)(2,1)}), bf16[2,2,88,352]{3,2,1,0:T(8,128)(2,1)S(1)}, u32[]{:S(2)}, u32[]{:S(2)}) %all-to-all-start.1) | async-done | bytes 247840 | tf_op jit(solution)/shard_map/all_to_all | solution.py:42
  43.5 3.4 %all-to-all-start.4 = ((bf16[2,2,88,352]{3,2,1,0:T(8,128)(2,1)}), bf16[2,2,88,352]{3,2,1,0:T(8,128)(2,1)S(1)}, u32[]{:S(2)}, u32[]{:S(2)}) async-start(bf16[2,2,88,352]{3,2,1,0:T(8,128)(2,1)} %bitcast.8), calls=%async_computation.4 | async-start | bytes 540672 | tf_op jit(solution)/shard_map/all_to_all | solution.py:42
  47.0 5.2 %all-to-all-done.4 = bf16[2,2,88,352]{3,2,1,0:T(8,128)(2,1)S(1)} async-done(((bf16[2,2,88,352]{3,2,1,0:T(8,128)(2,1)}), bf16[2,2,88,352]{3,2,1,0:T(8,128)(2,1)S(1)}, u32[]{:S(2)}, u32[]{:S(2)}) %all-to-all-start.4) | async-done | bytes 247840 | tf_op jit(solution)/shard_map/all_to_all | solution.py:42
  52.1 3.4 %all-to-all-start.7 = ((bf16[2,2,88,352]{3,2,1,0:T(8,128)(2,1)}), bf16[2,2,88,352]{3,2,1,0:T(8,128)(2,1)S(1)}, u32[]{:S(2)}, u32[]{:S(2)}) async-start(bf16[2,2,88,352]{3,2,1,0:T(8,128)(2,1)} %bitcast.15), calls=%async_computation.7 | async-start | bytes 540672 | tf_op jit(solution)/shard_map/all_to_all | solution.py:42
  55.6 0.1 broadcast_multiply_fusion.1
  55.6 0.7 copy.34
  56.4 4.4 %all-to-all-done.7 = bf16[2,2,88,352]{3,2,1,0:T(8,128)(2,1)S(1)} async-done(((bf16[2,2,88,352]{3,2,1,0:T(8,128)(2,1)}), bf16[2,2,88,352]{3,2,1,0:T(8,128)(2,1)S(1)}, u32[]{:S(2)}, u32[]{:S(2)}) %all-to-all-start.7) | async-done | bytes 247840 | tf_op jit(solution)/shard_map/all_to_all | solution.py:42
  60.8 5.1 %all-to-all-start.2 = ((bf16[4,1,1,88,352]{4,3,2,1,0:T(8,128)(2,1)}), bf16[4,1,1,88,352]{4,3,2,1,0:T(8,128)(2,1)S(1)}, u32[]{:S(2)}, u32[]{:S(2)}) async-start(bf16[4,1,1,88,352]{4,3,2,1,0:T(8,128)(2,1)} %bitcast.5), calls=%async_computation.2 | async-start | bytes 540672 | tf_op jit(solution)/shard_map/all_to_all | solution.py:50
  65.9 0.1 broadcast_multiply_fusion
  65.9 39.9 %psum.7 = f32[3,2,4,11]{3,2,1,0:T(4,128)S(1)} all-reduce(f32[3,2,4,11]{3,2,1,0:T(4,128)S(1)} %broadcast_multiply_fusion), channel_id=1, replica_groups=mesh['dp'=4,'pipe'=2,'tensor'=4] {'dp','pipe','tensor'}, use_global_device_ids=true, to_apply=%region_3.4 | all-reduce | flops 264 | bytes 2112 | tf_op jit(solution)/shard_map/psum | solution.py:77
  105.8 0.6 dynamic-slice_multiply_fusion
  106.4 0.7 copy.38
  107.1 0.7 copy.42
  107.9 0.0 all-to-all-done.2
  107.9 3.6 %all-to-all-start.5 = ((bf16[4,1,1,88,352]{4,3,2,1,0:T(8,128)(2,1)}), bf16[4,1,1,88,352]{4,3,2,1,0:T(8,128)(2,1)S(1)}, u32[]{:S(2)}, u32[]{:S(2)}) async-start(bf16[4,1,1,88,352]{4,3,2,1,0:T(8,128)(2,1)} %bitcast.12), calls=%async_computation.5 | async-start | bytes 540672 | tf_op jit(solution)/shard_map/all_to_all | solution.py:50
  111.4 0.2 copy.36
  111.6 11.0 %all_gather.9 = bf16[352,1408]{0,1:T(8,128)(2,1)S(1)} all-gather(bf16[352,352]{0,1:T(8,128)(2,1)S(1)} %copy.36), channel_id=1, replica_groups=mesh['dp'=4,'pipe'=2,'tensor'=4] {'dp'}, dimensions={1}, use_global_device_ids=true | all-gather | bytes 1239040 | tf_op jit(solution)/shard_map/all_gather | solution.py:56
  122.6 1.9 %copy.45 = bf16[352,1408]{1,0:T(8,128)(2,1)} copy(bf16[352,1408]{0,1:T(8,128)(2,1)S(1)} %all_gather.9) | data formatting | bytes 1982464
  124.5 0.0 all-to-all-done.5
  124.5 5.1 %all-to-all-start.8 = ((bf16[4,1,1,88,352]{4,3,2,1,0:T(8,128)(2,1)}), bf16[4,1,1,88,352]{4,3,2,1,0:T(8,128)(2,1)S(1)}, u32[]{:S(2)}, u32[]{:S(2)}) async-start(bf16[4,1,1,88,352]{4,3,2,1,0:T(8,128)(2,1)} %bitcast.19), calls=%async_computation.8 | async-start | bytes 540672 | tf_op jit(solution)/shard_map/all_to_all | solution.py:50
  129.6 0.2 copy.40
  129.8 10.0 %all_gather.10 = bf16[352,1408]{0,1:T(8,128)(2,1)S(1)} all-gather(bf16[352,352]{0,1:T(8,128)(2,1)S(1)} %copy.40), channel_id=1, replica_groups=mesh['dp'=4,'pipe'=2,'tensor'=4] {'dp'}, dimensions={1}, use_global_device_ids=true | all-gather | bytes 1239040 | tf_op jit(solution)/shard_map/all_gather | solution.py:56
  139.8 1.9 %copy.46 = bf16[352,1408]{1,0:T(8,128)(2,1)} copy(bf16[352,1408]{0,1:T(8,128)(2,1)S(1)} %all_gather.10) | data formatting | bytes 1982464
  141.7 0.0 all-to-all-done.8
  141.7 0.2 copy.44
  141.9 10.3 %all_gather.11 = bf16[352,1408]{0,1:T(8,128)(2,1)S(1)} all-gather(bf16[352,352]{0,1:T(8,128)(2,1)S(1)} %copy.44), channel_id=1, replica_groups=mesh['dp'=4,'pipe'=2,'tensor'=4] {'dp'}, dimensions={1}, use_global_device_ids=true | all-gather | bytes 1239040 | tf_op jit(solution)/shard_map/all_gather | solution.py:56
  152.2 1.9 %copy.47 = bf16[352,1408]{1,0:T(8,128)(2,1)} copy(bf16[352,1408]{0,1:T(8,128)(2,1)S(1)} %all_gather.11) | data formatting | bytes 1982464
  (9 shorter events, 0.0 us)
Async XLA Ops:
  0.6 27.4 %copy-start = (f32[1408]{0:T(1024)S(1)}, f32[1408]{0:T(1024)}, u32[]{:S(2)}) copy-start(f32[1408]{0:T(1024)} %param.8) | copy-start | bytes 16900
  0.6 6.4 %copy-start.3 = (bf16[88,1408]{1,0:T(8,128)(2,1)S(1)}, bf16[88,1408]{1,0:T(8,128)(2,1)}, u32[]{:S(2)}) copy-start(bf16[88,1408]{1,0:T(8,128)(2,1)} %param.6) | copy-start | bytes 743428
  2.7 15.2 %copy-start.2 = (bf16[88,1408]{1,0:T(8,128)(2,1)S(1)}, bf16[88,1408]{1,0:T(8,128)(2,1)}, u32[]{:S(2)}) copy-start(bf16[88,1408]{1,0:T(8,128)(2,1)} %param.7) | copy-start | bytes 743428
  2.7 11.0 %all-to-all-start = ((bf16[88,4,352]{2,0,1:T(8,128)(2,1)}), bf16[88,4,352]{2,0,1:T(8,128)(2,1)}, u32[]{:S(2)}, u32[]{:S(2)}) async-start(bf16[88,4,352]{2,0,1:T(8,128)(2,1)} %copy.33), calls=%async_computation | async-start | bytes 540672 | tf_op jit(solution)/shard_map/all_to_all | solution.py:33
  8.1 20.0 %copy-start.1 = (bf16[88,1408]{1,0:T(8,128)(2,1)S(1)}, bf16[88,1408]{1,0:T(8,128)(2,1)}, u32[]{:S(2)}) copy-start(bf16[88,1408]{1,0:T(8,128)(2,1)} %param.5) | copy-start | bytes 743428
  13.7 10.2 %all-to-all-start.3 = ((bf16[88,4,352]{2,0,1:T(8,128)(2,1)}), bf16[88,4,352]{2,0,1:T(8,128)(2,1)}, u32[]{:S(2)}, u32[]{:S(2)}) async-start(bf16[88,4,352]{2,0,1:T(8,128)(2,1)} %copy.37), calls=%async_computation.3 | async-start | bytes 540672 | tf_op jit(solution)/shard_map/all_to_all | solution.py:34
  18.1 20.0 %copy-start.4 = (f32[1408]{0:T(1024)S(1)}, f32[1408]{0:T(1024)}, u32[]{:S(2)}) copy-start(f32[1408]{0:T(1024)} %param.9) | copy-start | bytes 16900
  24.0 10.2 %all-to-all-start.6 = ((bf16[88,4,352]{2,0,1:T(8,128)(2,1)}), bf16[88,4,352]{2,0,1:T(8,128)(2,1)}, u32[]{:S(2)}, u32[]{:S(2)}) async-start(bf16[88,4,352]{2,0,1:T(8,128)(2,1)} %copy.41), calls=%async_computation.6 | async-start | bytes 540672 | tf_op jit(solution)/shard_map/all_to_all | solution.py:35
  34.2 9.3 %all-to-all-start.1 = ((bf16[2,2,88,352]{3,2,1,0:T(8,128)(2,1)}), bf16[2,2,88,352]{3,2,1,0:T(8,128)(2,1)S(1)}, u32[]{:S(2)}, u32[]{:S(2)}) async-start(bf16[2,2,88,352]{3,2,1,0:T(8,128)(2,1)} %bitcast.1), calls=%async_computation.1 | async-start | bytes 540672 | tf_op jit(solution)/shard_map/all_to_all | solution.py:42
  43.5 8.7 %all-to-all-start.4 = ((bf16[2,2,88,352]{3,2,1,0:T(8,128)(2,1)}), bf16[2,2,88,352]{3,2,1,0:T(8,128)(2,1)S(1)}, u32[]{:S(2)}, u32[]{:S(2)}) async-start(bf16[2,2,88,352]{3,2,1,0:T(8,128)(2,1)} %bitcast.8), calls=%async_computation.4 | async-start | bytes 540672 | tf_op jit(solution)/shard_map/all_to_all | solution.py:42
  52.1 8.7 %all-to-all-start.7 = ((bf16[2,2,88,352]{3,2,1,0:T(8,128)(2,1)}), bf16[2,2,88,352]{3,2,1,0:T(8,128)(2,1)S(1)}, u32[]{:S(2)}, u32[]{:S(2)}) async-start(bf16[2,2,88,352]{3,2,1,0:T(8,128)(2,1)} %bitcast.15), calls=%async_computation.7 | async-start | bytes 540672 | tf_op jit(solution)/shard_map/all_to_all | solution.py:42
  60.8 47.1 %all-to-all-start.2 = ((bf16[4,1,1,88,352]{4,3,2,1,0:T(8,128)(2,1)}), bf16[4,1,1,88,352]{4,3,2,1,0:T(8,128)(2,1)S(1)}, u32[]{:S(2)}, u32[]{:S(2)}) async-start(bf16[4,1,1,88,352]{4,3,2,1,0:T(8,128)(2,1)} %bitcast.5), calls=%async_computation.2 | async-start | bytes 540672 | tf_op jit(solution)/shard_map/all_to_all | solution.py:50
  107.9 16.6 %all-to-all-start.5 = ((bf16[4,1,1,88,352]{4,3,2,1,0:T(8,128)(2,1)}), bf16[4,1,1,88,352]{4,3,2,1,0:T(8,128)(2,1)S(1)}, u32[]{:S(2)}, u32[]{:S(2)}) async-start(bf16[4,1,1,88,352]{4,3,2,1,0:T(8,128)(2,1)} %bitcast.12), calls=%async_computation.5 | async-start | bytes 540672 | tf_op jit(solution)/shard_map/all_to_all | solution.py:50
  124.5 17.2 %all-to-all-start.8 = ((bf16[4,1,1,88,352]{4,3,2,1,0:T(8,128)(2,1)}), bf16[4,1,1,88,352]{4,3,2,1,0:T(8,128)(2,1)S(1)}, u32[]{:S(2)}, u32[]{:S(2)}) async-start(bf16[4,1,1,88,352]{4,3,2,1,0:T(8,128)(2,1)} %bitcast.19), calls=%async_computation.8 | async-start | bytes 540672 | tf_op jit(solution)/shard_map/all_to_all | solution.py:50
where the time goes:
time: 155 us; the launch traced here: 154 us
  blocking collectives  71.2 us (46%)
  starting transfers between devices  36.7 us (24%)
  waiting for transfers between devices  31 us (20%)
  local copies, waits for them, and re-layouts  12.5 us (8%)
    psum x1, blocking collectives, shards(): summed = lax.psum(spread, ('dp', 'pipe', 'tensor'))  39.9 us
    all_gather x3, blocking collectives, shards(): lax.all_gather(for_sending(flat_pieces), 'dp', axis=1, tiled=True)  31.3 us
    all_to_all x3, waiting for transfers between devices, shards(): lax.all_to_all(for_sending(grouped), 'pipe', split_axis=0, concat_axis=2,...  14.7 us
    all_to_all x3, starting transfers between devices, shards(): lax.all_to_all(for_sending(routed), 'tensor', split_axis=0, concat_axis=2...  13.7 us
    all_to_all x3, starting transfers between devices, shards(): lax.all_to_all(for_sending(grouped), 'pipe', split_axis=0, concat_axis=2,...  10.5 us
    unnamed x13, local copies, waits for them, and re-layouts  5.65 us
    all_to_all x1, waiting for transfers between devices, shards(): lax.all_to_all(sources[0], 'dp', split_axis=1, concat_axis=0, tiled=True)  5.65 us
    all_to_all x1, waiting for transfers between devices, shards(): lax.all_to_all(sources[2], 'dp', split_axis=1, concat_axis=0, tiled=True)  5.51 us
  transfers between devices with their start and end apart: 9, of which 6 were waited for; matrix products, arithmetic and copies ran while one was open for 6% of the time, Pallas kernels for 0%

commit v1 on v0

--- a/solution.py
+++ b/solution.py
@@ -74,7 +74,7 @@
         * section_hit[None, :, None, None]
         * tile_hit[None, None, :, None]
     )
-    summed = lax.psum(spread, ("dp", "pipe", "tensor"))
+    summed = lax.psum(lax.psum(spread, "dp"), ("pipe", "tensor"))
     checks = (
         lax.dynamic_slice(summed, (0, lax.axis_index("pipe"), tensor_pos, 0), (3, 1, 1, col_blocks))
         * factor

time: 155 us -> 160 us (1.032)
  blocking collectives: 71.2 us -> 76.4 us
    psum x1 -> x2, blocking collectives: 39.9 us -> 46.7 us  [shards(): summed = lax.psum(lax.psum(spread, 'dp'), ('pipe', 'tensor'))]
where the time goes in v1:
time: 160 us; the launch traced here: 159 us
  blocking collectives  76.4 us (48%)
  starting transfers between devices  36.6 us (23%)
  waiting for transfers between devices  31 us (19%)
  local copies, waits for them, and re-layouts  12.5 us (8%)
    psum x2, blocking collectives, shards(): summed = lax.psum(lax.psum(spread, 'dp'), ('pipe', 'tensor'))  46.7 us
    all_gather x3, blocking collectives, shards(): lax.all_gather(for_sending(flat_pieces), 'dp', axis=1, tiled=True)  29.8 us
    all_to_all x3, waiting for transfers between devices, shards(): lax.all_to_all(for_sending(grouped), 'pipe', split_axis=0, concat_axis=2,...  14.7 us
    all_to_all x3, starting transfers between devices, shards(): lax.all_to_all(for_sending(routed), 'tensor', split_axis=0, concat_axis=2...  13.6 us
    all_to_all x3, starting transfers between devices, shards(): lax.all_to_all(for_sending(grouped), 'pipe', split_axis=0, concat_axis=2,...  10.5 us
    all_to_all x1, waiting for transfers between devices, shards(): lax.all_to_all(sources[0], 'dp', split_axis=1, concat_axis=0, tiled=True)  5.65 us
    unnamed x13, local copies, waits for them, and re-layouts  5.65 us
    all_to_all x1, waiting for transfers between devices, shards(): lax.all_to_all(sources[2], 'dp', split_axis=1, concat_axis=0, tiled=True)  5.51 us
  transfers between devices with their start and end apart: 9, of which 6 were waited for; matrix products, arithmetic and copies ran while one was open for 6% of the time, Pallas kernels for 0%

profile of v1, /device:TPU:0, one launch (start us, length us, event | category | flops | bytes accessed | tf_op | source)
XLA Modules:
  0.0 159.2 jit_solution(6410789803808654309)
XLA Ops:
  0.6 0.0 copy-start
  0.7 1.3 all_to_all.90
  1.9 0.7 copy.33
  2.7 4.4 %all-to-all-start = ((bf16[88,4,352]{2,0,1:T(8,128)(2,1)}), bf16[88,4,352]{2,0,1:T(8,128)(2,1)}, u32[]{:S(2)}, u32[]{:S(2)}) async-start(bf16[88,4,352]{2,0,1:T(8,128)(2,1)} %copy.33), calls=%async_computation | async-start | bytes 540672 | tf_op jit(solution)/shard_map/all_to_all | solution.py:33
  7.0 0.3 all_to_all.97
  7.3 0.7 copy.37
  8.1 5.7 %all-to-all-done = bf16[88,4,352]{2,0,1:T(8,128)(2,1)} async-done(((bf16[88,4,352]{2,0,1:T(8,128)(2,1)}), bf16[88,4,352]{2,0,1:T(8,128)(2,1)}, u32[]{:S(2)}, u32[]{:S(2)}) %all-to-all-start) | async-done | bytes 247840 | tf_op jit(solution)/shard_map/all_to_all | solution.py:33
  13.7 4.1 %all-to-all-start.3 = ((bf16[88,4,352]{2,0,1:T(8,128)(2,1)}), bf16[88,4,352]{2,0,1:T(8,128)(2,1)}, u32[]{:S(2)}, u32[]{:S(2)}) async-start(bf16[88,4,352]{2,0,1:T(8,128)(2,1)} %copy.37), calls=%async_computation.3 | async-start | bytes 540672 | tf_op jit(solution)/shard_map/all_to_all | solution.py:34
  17.9 0.3 all_to_all.104
  18.1 0.0 copy-start.4
  18.2 0.7 copy.41
  18.9 5.1 %all-to-all-done.3 = bf16[88,4,352]{2,0,1:T(8,128)(2,1)} async-done(((bf16[88,4,352]{2,0,1:T(8,128)(2,1)}), bf16[88,4,352]{2,0,1:T(8,128)(2,1)}, u32[]{:S(2)}, u32[]{:S(2)}) %all-to-all-start.3) | async-done | bytes 247840 | tf_op jit(solution)/shard_map/all_to_all | solution.py:34
  24.0 4.1 %all-to-all-start.6 = ((bf16[88,4,352]{2,0,1:T(8,128)(2,1)}), bf16[88,4,352]{2,0,1:T(8,128)(2,1)}, u32[]{:S(2)}, u32[]{:S(2)}) async-start(bf16[88,4,352]{2,0,1:T(8,128)(2,1)} %copy.41), calls=%async_computation.6 | async-start | bytes 540672 | tf_op jit(solution)/shard_map/all_to_all | solution.py:35
  28.1 0.0 copy-done
  28.1 0.3 convolution_reduce_fusion.2
  28.4 0.3 convolution_reduce_fusion
  28.7 5.5 %all-to-all-done.6 = bf16[88,4,352]{2,0,1:T(8,128)(2,1)} async-done(((bf16[88,4,352]{2,0,1:T(8,128)(2,1)}), bf16[88,4,352]{2,0,1:T(8,128)(2,1)}, u32[]{:S(2)}, u32[]{:S(2)}) %all-to-all-start.6) | async-done | bytes 247840 | tf_op jit(solution)/shard_map/all_to_all | solution.py:35
  34.2 3.6 %all-to-all-start.1 = ((bf16[2,2,88,352]{3,2,1,0:T(8,128)(2,1)}), bf16[2,2,88,352]{3,2,1,0:T(8,128)(2,1)S(1)}, u32[]{:S(2)}, u32[]{:S(2)}) async-start(bf16[2,2,88,352]{3,2,1,0:T(8,128)(2,1)} %bitcast.1), calls=%async_computation.1 | async-start | bytes 540672 | tf_op jit(solution)/shard_map/all_to_all | solution.py:42
  37.8 0.3 convolution_reduce_fusion.1
  38.1 0.1 bitcast_reduce_fusion.2
  38.3 5.2 %all-to-all-done.1 = bf16[2,2,88,352]{3,2,1,0:T(8,128)(2,1)S(1)} async-done(((bf16[2,2,88,352]{3,2,1,0:T(8,128)(2,1)}), bf16[2,2,88,352]{3,2,1,0:T(8,128)(2,1)S(1)}, u32[]{:S(2)}, u32[]{:S(2)}) %all-to-all-start.1) | async-done | bytes 247840 | tf_op jit(solution)/shard_map/all_to_all | solution.py:42
  43.5 3.4 %all-to-all-start.4 = ((bf16[2,2,88,352]{3,2,1,0:T(8,128)(2,1)}), bf16[2,2,88,352]{3,2,1,0:T(8,128)(2,1)S(1)}, u32[]{:S(2)}, u32[]{:S(2)}) async-start(bf16[2,2,88,352]{3,2,1,0:T(8,128)(2,1)} %bitcast.8), calls=%async_computation.4 | async-start | bytes 540672 | tf_op jit(solution)/shard_map/all_to_all | solution.py:42
  47.0 5.2 %all-to-all-done.4 = bf16[2,2,88,352]{3,2,1,0:T(8,128)(2,1)S(1)} async-done(((bf16[2,2,88,352]{3,2,1,0:T(8,128)(2,1)}), bf16[2,2,88,352]{3,2,1,0:T(8,128)(2,1)S(1)}, u32[]{:S(2)}, u32[]{:S(2)}) %all-to-all-start.4) | async-done | bytes 247840 | tf_op jit(solution)/shard_map/all_to_all | solution.py:42
  52.1 3.4 %all-to-all-start.7 = ((bf16[2,2,88,352]{3,2,1,0:T(8,128)(2,1)}), bf16[2,2,88,352]{3,2,1,0:T(8,128)(2,1)S(1)}, u32[]{:S(2)}, u32[]{:S(2)}) async-start(bf16[2,2,88,352]{3,2,1,0:T(8,128)(2,1)} %bitcast.15), calls=%async_computation.7 | async-start | bytes 540672 | tf_op jit(solution)/shard_map/all_to_all | solution.py:42
  55.6 0.1 broadcast_multiply_fusion.1
  55.7 0.7 copy.34
  56.4 4.4 %all-to-all-done.7 = bf16[2,2,88,352]{3,2,1,0:T(8,128)(2,1)S(1)} async-done(((bf16[2,2,88,352]{3,2,1,0:T(8,128)(2,1)}), bf16[2,2,88,352]{3,2,1,0:T(8,128)(2,1)S(1)}, u32[]{:S(2)}, u32[]{:S(2)}) %all-to-all-start.7) | async-done | bytes 247840 | tf_op jit(solution)/shard_map/all_to_all | solution.py:42
  60.8 5.1 %all-to-all-start.2 = ((bf16[4,1,1,88,352]{4,3,2,1,0:T(8,128)(2,1)}), bf16[4,1,1,88,352]{4,3,2,1,0:T(8,128)(2,1)S(1)}, u32[]{:S(2)}, u32[]{:S(2)}) async-start(bf16[4,1,1,88,352]{4,3,2,1,0:T(8,128)(2,1)} %bitcast.5), calls=%async_computation.2 | async-start | bytes 540672 | tf_op jit(solution)/shard_map/all_to_all | solution.py:50
  65.9 0.1 broadcast_multiply_fusion
  66.0 10.4 %psum.14 = f32[3,2,4,11]{3,2,1,0:T(4,128)S(1)} all-reduce(f32[3,2,4,11]{3,2,1,0:T(4,128)S(1)} %broadcast_multiply_fusion), channel_id=1, replica_groups=mesh['dp'=4,'pipe'=2,'tensor'=4] {'dp'}, use_global_device_ids=true, to_apply=%region_3.4 | all-reduce | flops 264 | bytes 2112 | tf_op jit(solution)/shard_map/psum | solution.py:77
  76.4 36.2 %psum.15 = f32[3,2,4,11]{3,2,1,0:T(4,128)S(1)} all-reduce(f32[3,2,4,11]{3,2,1,0:T(4,128)S(1)} %psum.14), channel_id=1, replica_groups=mesh['dp'=4,'pipe'=2,'tensor'=4] {'pipe','tensor'}, use_global_device_ids=true, to_apply=%region_4.5 | all-reduce | flops 264 | bytes 2112 | tf_op jit(solution)/shard_map/psum | solution.py:77
  112.6 0.6 dynamic-slice_multiply_fusion
  113.2 0.7 copy.38
  113.9 0.7 copy.42
  114.7 0.0 all-to-all-done.2
  114.7 3.5 %all-to-all-start.5 = ((bf16[4,1,1,88,352]{4,3,2,1,0:T(8,128)(2,1)}), bf16[4,1,1,88,352]{4,3,2,1,0:T(8,128)(2,1)S(1)}, u32[]{:S(2)}, u32[]{:S(2)}) async-start(bf16[4,1,1,88,352]{4,3,2,1,0:T(8,128)(2,1)} %bitcast.12), calls=%async_computation.5 | async-start | bytes 540672 | tf_op jit(solution)/shard_map/all_to_all | solution.py:50
  118.1 0.2 copy.36
  118.3 9.3 %all_gather.9 = bf16[352,1408]{0,1:T(8,128)(2,1)S(1)} all-gather(bf16[352,352]{0,1:T(8,128)(2,1)S(1)} %copy.36), channel_id=1, replica_groups=mesh['dp'=4,'pipe'=2,'tensor'=4] {'dp'}, dimensions={1}, use_global_device_ids=true | all-gather | bytes 1239040 | tf_op jit(solution)/shard_map/all_gather | solution.py:56
  127.7 1.9 %copy.45 = bf16[352,1408]{1,0:T(8,128)(2,1)} copy(bf16[352,1408]{0,1:T(8,128)(2,1)S(1)} %all_gather.9) | data formatting | bytes 1982464
  129.6 0.0 all-to-all-done.5
  129.6 5.1 %all-to-all-start.8 = ((bf16[4,1,1,88,352]{4,3,2,1,0:T(8,128)(2,1)}), bf16[4,1,1,88,352]{4,3,2,1,0:T(8,128)(2,1)S(1)}, u32[]{:S(2)}, u32[]{:S(2)}) async-start(bf16[4,1,1,88,352]{4,3,2,1,0:T(8,128)(2,1)} %bitcast.19), calls=%async_computation.8 | async-start | bytes 540672 | tf_op jit(solution)/shard_map/all_to_all | solution.py:50
  134.6 0.2 copy.40
  134.8 10.1 %all_gather.10 = bf16[352,1408]{0,1:T(8,128)(2,1)S(1)} all-gather(bf16[352,352]{0,1:T(8,128)(2,1)S(1)} %copy.40), channel_id=1, replica_groups=mesh['dp'=4,'pipe'=2,'tensor'=4] {'dp'}, dimensions={1}, use_global_device_ids=true | all-gather | bytes 1239040 | tf_op jit(solution)/shard_map/all_gather | solution.py:56
  144.9 1.9 %copy.46 = bf16[352,1408]{1,0:T(8,128)(2,1)} copy(bf16[352,1408]{0,1:T(8,128)(2,1)S(1)} %all_gather.10) | data formatting | bytes 1982464
  146.8 0.0 all-to-all-done.8
  146.8 0.2 copy.44
  147.0 10.3 %all_gather.11 = bf16[352,1408]{0,1:T(8,128)(2,1)S(1)} all-gather(bf16[352,352]{0,1:T(8,128)(2,1)S(1)} %copy.44), channel_id=1, replica_groups=mesh['dp'=4,'pipe'=2,'tensor'=4] {'dp'}, dimensions={1}, use_global_device_ids=true | all-gather | bytes 1239040 | tf_op jit(solution)/shard_map/all_gather | solution.py:56
  157.3 1.9 %copy.47 = bf16[352,1408]{1,0:T(8,128)(2,1)} copy(bf16[352,1408]{0,1:T(8,128)(2,1)S(1)} %all_gather.11) | data formatting | bytes 1982464
  (10 shorter events, 0.0 us)
Async XLA Ops:
  0.6 27.4 %copy-start = (f32[1408]{0:T(1024)S(1)}, f32[1408]{0:T(1024)}, u32[]{:S(2)}) copy-start(f32[1408]{0:T(1024)} %param.8) | copy-start | bytes 16900
  0.6 6.4 %copy-start.3 = (bf16[88,1408]{1,0:T(8,128)(2,1)S(1)}, bf16[88,1408]{1,0:T(8,128)(2,1)}, u32[]{:S(2)}) copy-start(bf16[88,1408]{1,0:T(8,128)(2,1)} %param.6) | copy-start | bytes 743428
  2.7 15.2 %copy-start.2 = (bf16[88,1408]{1,0:T(8,128)(2,1)S(1)}, bf16[88,1408]{1,0:T(8,128)(2,1)}, u32[]{:S(2)}) copy-start(bf16[88,1408]{1,0:T(8,128)(2,1)} %param.7) | copy-start | bytes 743428
  2.7 11.1 %all-to-all-start = ((bf16[88,4,352]{2,0,1:T(8,128)(2,1)}), bf16[88,4,352]{2,0,1:T(8,128)(2,1)}, u32[]{:S(2)}, u32[]{:S(2)}) async-start(bf16[88,4,352]{2,0,1:T(8,128)(2,1)} %copy.33), calls=%async_computation | async-start | bytes 540672 | tf_op jit(solution)/shard_map/all_to_all | solution.py:33
  8.1 20.0 %copy-start.1 = (bf16[88,1408]{1,0:T(8,128)(2,1)S(1)}, bf16[88,1408]{1,0:T(8,128)(2,1)}, u32[]{:S(2)}) copy-start(bf16[88,1408]{1,0:T(8,128)(2,1)} %param.5) | copy-start | bytes 743428
  13.7 10.3 %all-to-all-start.3 = ((bf16[88,4,352]{2,0,1:T(8,128)(2,1)}), bf16[88,4,352]{2,0,1:T(8,128)(2,1)}, u32[]{:S(2)}, u32[]{:S(2)}) async-start(bf16[88,4,352]{2,0,1:T(8,128)(2,1)} %copy.37), calls=%async_computation.3 | async-start | bytes 540672 | tf_op jit(solution)/shard_map/all_to_all | solution.py:34
  18.1 20.0 %copy-start.4 = (f32[1408]{0:T(1024)S(1)}, f32[1408]{0:T(1024)}, u32[]{:S(2)}) copy-start(f32[1408]{0:T(1024)} %param.9) | copy-start | bytes 16900
  24.0 10.2 %all-to-all-start.6 = ((bf16[88,4,352]{2,0,1:T(8,128)(2,1)}), bf16[88,4,352]{2,0,1:T(8,128)(2,1)}, u32[]{:S(2)}, u32[]{:S(2)}) async-start(bf16[88,4,352]{2,0,1:T(8,128)(2,1)} %copy.41), calls=%async_computation.6 | async-start | bytes 540672 | tf_op jit(solution)/shard_map/all_to_all | solution.py:35
  34.2 9.3 %all-to-all-start.1 = ((bf16[2,2,88,352]{3,2,1,0:T(8,128)(2,1)}), bf16[2,2,88,352]{3,2,1,0:T(8,128)(2,1)S(1)}, u32[]{:S(2)}, u32[]{:S(2)}) async-start(bf16[2,2,88,352]{3,2,1,0:T(8,128)(2,1)} %bitcast.1), calls=%async_computation.1 | async-start | bytes 540672 | tf_op jit(solution)/shard_map/all_to_all | solution.py:42
  43.5 8.7 %all-to-all-start.4 = ((bf16[2,2,88,352]{3,2,1,0:T(8,128)(2,1)}), bf16[2,2,88,352]{3,2,1,0:T(8,128)(2,1)S(1)}, u32[]{:S(2)}, u32[]{:S(2)}) async-start(bf16[2,2,88,352]{3,2,1,0:T(8,128)(2,1)} %bitcast.8), calls=%async_computation.4 | async-start | bytes 540672 | tf_op jit(solution)/shard_map/all_to_all | solution.py:42
  52.1 8.7 %all-to-all-start.7 = ((bf16[2,2,88,352]{3,2,1,0:T(8,128)(2,1)}), bf16[2,2,88,352]{3,2,1,0:T(8,128)(2,1)S(1)}, u32[]{:S(2)}, u32[]{:S(2)}) async-start(bf16[2,2,88,352]{3,2,1,0:T(8,128)(2,1)} %bitcast.15), calls=%async_computation.7 | async-start | bytes 540672 | tf_op jit(solution)/shard_map/all_to_all | solution.py:42
  60.8 53.9 %all-to-all-start.2 = ((bf16[4,1,1,88,352]{4,3,2,1,0:T(8,128)(2,1)}), bf16[4,1,1,88,352]{4,3,2,1,0:T(8,128)(2,1)S(1)}, u32[]{:S(2)}, u32[]{:S(2)}) async-start(bf16[4,1,1,88,352]{4,3,2,1,0:T(8,128)(2,1)} %bitcast.5), calls=%async_computation.2 | async-start | bytes 540672 | tf_op jit(solution)/shard_map/all_to_all | solution.py:50
  114.7 14.9 %all-to-all-start.5 = ((bf16[4,1,1,88,352]{4,3,2,1,0:T(8,128)(2,1)}), bf16[4,1,1,88,352]{4,3,2,1,0:T(8,128)(2,1)S(1)}, u32[]{:S(2)}, u32[]{:S(2)}) async-start(bf16[4,1,1,88,352]{4,3,2,1,0:T(8,128)(2,1)} %bitcast.12), calls=%async_computation.5 | async-start | bytes 540672 | tf_op jit(solution)/shard_map/all_to_all | solution.py:50
  129.6 17.2 %all-to-all-start.8 = ((bf16[4,1,1,88,352]{4,3,2,1,0:T(8,128)(2,1)}), bf16[4,1,1,88,352]{4,3,2,1,0:T(8,128)(2,1)S(1)}, u32[]{:S(2)}, u32[]{:S(2)}) async-start(bf16[4,1,1,88,352]{4,3,2,1,0:T(8,128)(2,1)} %bitcast.19), calls=%async_computation.8 | async-start | bytes 540672 | tf_op jit(solution)/shard_map/all_to_all | solution.py:50
